TPU v7x, 32 devices: a whole 2x2x4 slice. The times are simulated.
32 devices in a mesh: dp: 4 (over y, core), tensor: 8 (over z, x).
Axes of the slice: x: 2, y: 2, z: 4, core: 2. Of those that a mesh axis runs over, the one named last changes fastest.
Arguments:
- ref_hidden: bfloat16 [1152, 4608], P('dp', 'tensor'), may hold values from -6 to 6
- pol_hidden: bfloat16 [1152, 4608], P('dp', 'tensor'), may hold values from -6 to 6
- readout: bfloat16 [1152, 4608], P('dp', 'tensor'), may hold values from -0.019897461 to 0.019897461
- lengths: int32 [12], P('dp'), may hold values from 16 to 96, as said below
- pairing: int32 [12], replicated, may hold values from 0 to 11, each once
- pre_gain: float32 [4608], replicated, may hold values from 0.25 to 1.75
- post_gain: float32 [4608], replicated, may hold values from 0.25 to 1.75
- w_query: bfloat16 [4608, 4096], P('dp', 'tensor'), may hold values from -0.09375 to 0.09375
- w_key: bfloat16 [4608, 2048], P('dp', 'tensor'), may hold values from -3 to 3
- value_projection: bfloat16 [4608, 2048], P('dp', 'tensor'), may hold values from -0.09375 to 0.09375
- w_out: bfloat16 [4608, 4096], P('dp', 'tensor'), may hold values from -0.09375 to 0.09375
- a_query: bfloat16 [4608, 64], P('dp'), may hold values from -0.09375 to 0.09375
- a_value: bfloat16 [4608, 64], P('dp'), may hold values from -0.09375 to 0.09375
- query_second_factor: bfloat16 [64, 4096], P(None, 'tensor'), may hold values from -0.75 to 0.75
- value_second_factor: bfloat16 [64, 2048], P(None, 'tensor'), may hold values from -0.75 to 0.75
Outputs:
- policy_out: bfloat16 [1152, 4608], P('dp', 'tensor')
- reference_out: bfloat16 [1152, 4608], P('dp', 'tensor')
- dpo_loss: float32 [], replicated
- grad_hidden: bfloat16 [1152, 4608], P('dp', 'tensor')
- grad_a: float32 [4608, 128], P('dp')
- query_factor_gradient: float32 [64, 4096], P(None, 'tensor')
- value_factor_gradient: float32 [64, 2048], P(None, 'tensor')
Inputs may be any that keep to these rules, and one draw needn't show every extreme that they name: `lengths`: every sequence has at least one valid token and some sequence is full. `pairing`: entries 2k and 2k + 1 name the chosen and the rejected sequence of pair k; every sequence appears once.
All inputs are finite; a program needn't handle non-finite values.
Results may differ from a plain program's by a relative error of at most 0.0233.
The roundings to bfloat16 on the way count: a program that leaves them out, or rounds other values in their place, can miss the bound.
Values may be sent and summed in bfloat16 or wider, within the bound.
A program may use at most 128 MiB of HBM per device.

v0:
```python
import jax
import jax.numpy as jnp
from jax import lax
from jax.sharding import PartitionSpec as P

MODEL_WIDTH = 4608
HQ = 32
HEAD_SIZE = 128
NORM_EPS = 1e-06
SOFT_CAP = 50.0
ADAPTER_SCALE = 0.5
DPO_BETA = 0.5
LOSS_SCALE = 256.0
ROPE_BASE = 10000.0


def query_scale():
    return float(MODEL_WIDTH // HQ) ** (-0.5)


def apply_rotation(value_rows, direction):
    length = value_rows.shape[1]
    head_depth = value_rows.shape[3]
    middle = head_depth // 2
    spacing = ROPE_BASE ** (-2.0 * jnp.arange(middle, dtype=jnp.float32) / head_depth)
    angles = jnp.arange(length, dtype=jnp.float32)[:, None] * spacing[None, :]
    cosine = jnp.cos(angles)[None, :, None, :]
    sine_part = direction * jnp.sin(angles)[None, :, None, :]
    leading = value_rows[..., :middle]
    trailing = value_rows[..., middle:]
    return jnp.concatenate(
        [leading * cosine - trailing * sine_part, trailing * cosine + leading * sine_part], axis=-1
    )


def allowed_mask(lengths, length):
    places = jnp.arange(length)
    causal = places[None, :] <= places[:, None]
    living = places[None, :] < lengths[:, None]
    return causal[None, None, None, :, :] & living[:, None, None, None, :]


def attend(query_rows, rotated_keys, value_rows, lengths):
    seqs_here, length, q_heads, head_depth = query_rows.shape
    kv_heads = rotated_keys.shape[2]
    grouped_heads = query_rows.reshape(seqs_here, length, kv_heads, q_heads // kv_heads, head_depth)
    scores = (
        jnp.einsum(
            "sqkgd,spkd->skgqp", grouped_heads, rotated_keys, preferred_element_type=jnp.float32
        )
        * query_scale()
    )
    capped = SOFT_CAP * jnp.tanh(scores / SOFT_CAP)
    allowed = allowed_mask(lengths, length)
    weights = jnp.where(allowed, jnp.exp(capped), 0.0)
    probabilities = weights / jnp.sum(weights, axis=-1, keepdims=True)
    probs_low = probabilities.astype(jnp.bfloat16)
    mixed_out = jnp.einsum(
        "skgqp,spkd->sqkgd", probs_low, value_rows, preferred_element_type=jnp.float32
    )
    return (
        mixed_out.astype(jnp.bfloat16).reshape(seqs_here, length, q_heads, head_depth),
        probs_low,
        probabilities,
        capped,
    )


def attend_back(grad_mixed, query_rows, rotated_keys, value_rows, probs_low, probabilities, capped):
    seqs_here, length, q_heads, head_depth = query_rows.shape
    kv_heads = rotated_keys.shape[2]
    shape_five = (seqs_here, length, kv_heads, q_heads // kv_heads, head_depth)
    grouped_heads = query_rows.reshape(shape_five)
    grad_grouped = grad_mixed.reshape(shape_five)
    grad_probs = jnp.einsum(
        "sqkgd,spkd->skgqp", grad_grouped, value_rows, preferred_element_type=jnp.float32
    )
    value_rows_gradient = jnp.einsum(
        "skgqp,sqkgd->spkd", probs_low, grad_grouped, preferred_element_type=jnp.float32
    )
    centered = grad_probs - jnp.sum(grad_probs * probabilities, axis=-1, keepdims=True)
    grad_scores = (
        probabilities * centered * (1.0 - (capped / SOFT_CAP) ** 2) * query_scale()
    ).astype(jnp.bfloat16)
    query_rows_gradient = jnp.einsum(
        "skgqp,spkd->sqkgd", grad_scores, rotated_keys, preferred_element_type=jnp.float32
    ).reshape(seqs_here, length, q_heads, head_depth)
    key_rows_gradient = jnp.einsum(
        "skgqp,sqkgd->spkd", grad_scores, grouped_heads, preferred_element_type=jnp.float32
    )
    return (query_rows_gradient, key_rows_gradient, value_rows_gradient)


def normalize(hidden, pre_gain):
    whole_rows = lax.all_gather(hidden, "tensor", axis=1, tiled=True)
    wide_rows = whole_rows.astype(jnp.float32)
    pre_scale = lax.rsqrt(
        jnp.sum(wide_rows * wide_rows, axis=1, keepdims=True) / pre_gain.shape[0] + NORM_EPS
    )
    normed = (wide_rows * pre_scale * pre_gain).astype(jnp.bfloat16)
    return (normed, pre_scale)


def attention_layer(hidden, normed, weights, adapters, lengths, post_local):
    w_query, w_key, value_projection, w_out, a_query, a_value = weights
    tok_rows, full_width = normed.shape
    seqs_here = lengths.shape[0]
    length = tok_rows // seqs_here
    query_rows = jnp.dot(normed, w_query, preferred_element_type=jnp.float32)
    keys_before_rotation = jnp.dot(normed, w_key, preferred_element_type=jnp.float32)
    value_rows = jnp.dot(normed, value_projection, preferred_element_type=jnp.float32)
    low_rank_update = None
    if adapters is not None:
        query_second_factor, value_second_factor = adapters
        rank_size = query_second_factor.shape[0]
        low_rank_update = jnp.dot(
            normed, jnp.concatenate([a_query, a_value], axis=1), preferred_element_type=jnp.float32
        ).astype(jnp.bfloat16)
        query_rows = query_rows + ADAPTER_SCALE * jnp.dot(
            low_rank_update[:, :rank_size], query_second_factor, preferred_element_type=jnp.float32
        )
        value_rows = value_rows + ADAPTER_SCALE * jnp.dot(
            low_rank_update[:, rank_size:], value_second_factor, preferred_element_type=jnp.float32
        )
    q_heads = query_rows.shape[1] // HEAD_SIZE
    kv_heads = keys_before_rotation.shape[1] // HEAD_SIZE
    query_rows = apply_rotation(
        query_rows.reshape(seqs_here, length, q_heads, HEAD_SIZE), 1.0
    ).astype(jnp.bfloat16)
    rotated_keys = apply_rotation(
        keys_before_rotation.reshape(seqs_here, length, kv_heads, HEAD_SIZE), 1.0
    ).astype(jnp.bfloat16)
    value_rows = value_rows.reshape(seqs_here, length, kv_heads, HEAD_SIZE).astype(jnp.bfloat16)
    mixed_out, probs_low, probabilities, capped = attend(
        query_rows, rotated_keys, value_rows, lengths
    )
    head_terms = lax.dot_general(
        mixed_out.reshape(tok_rows, q_heads * HEAD_SIZE),
        w_out,
        (((1,), (1,)), ((), ())),
        preferred_element_type=jnp.float32,
    )
    summed = lax.psum_scatter(
        head_terms.astype(jnp.bfloat16), "tensor", scatter_dimension=1, tiled=True
    ).astype(jnp.float32)
    squares = lax.psum(jnp.sum(summed * summed, axis=1), "tensor")
    post_scale = lax.rsqrt(squares[:, None] / full_width + NORM_EPS)
    result = hidden.astype(jnp.float32) + summed * post_scale * post_local
    saved = (
        low_rank_update,
        query_rows,
        rotated_keys,
        value_rows,
        probs_low,
        probabilities,
        capped,
        summed,
        post_scale,
    )
    return (result, saved)


def body(
    ref_hidden,
    pol_hidden,
    readout,
    lengths,
    pairing,
    pre_gain,
    post_gain,
    w_query,
    w_key,
    value_projection,
    w_out,
    a_query,
    a_value,
    query_second_factor,
    value_second_factor,
):
    tok_rows, part_width = pol_hidden.shape
    seqs_here = lengths.shape[0]
    length = tok_rows // seqs_here
    tensor_rank = lax.axis_index("tensor")
    data_rank = lax.axis_index("dp")
    all_seqs = seqs_here * lax.axis_size("dp")
    full_width = part_width * lax.axis_size("tensor")
    pre_local = lax.dynamic_slice_in_dim(pre_gain, tensor_rank * part_width, part_width)
    post_local = lax.dynamic_slice_in_dim(post_gain, tensor_rank * part_width, part_width)
    weights = (
        lax.all_gather(w_query, "dp", axis=0, tiled=True),
        lax.all_gather(w_key, "dp", axis=0, tiled=True),
        lax.all_gather(value_projection, "dp", axis=0, tiled=True),
        lax.all_gather(w_out, "dp", axis=0, tiled=True),
        lax.all_gather(a_query, "dp", axis=0, tiled=True),
        lax.all_gather(a_value, "dp", axis=0, tiled=True),
    )
    w_query_all, w_key_all, w_value_all, w_out_all, a_query_all, a_value_all = weights
    ref_normed, ref_scale = normalize(ref_hidden, pre_gain)
    ref_result, ref_saved = attention_layer(
        ref_hidden, ref_normed, weights, None, lengths, post_local
    )
    pol_normed, pol_scale = normalize(pol_hidden, pre_gain)
    pol_result, pol_saved = attention_layer(
        pol_hidden,
        pol_normed,
        weights,
        (query_second_factor, value_second_factor),
        lengths,
        post_local,
    )
    readout_wide = readout.astype(jnp.float32)
    living = (jnp.arange(length)[None, :] < lengths[:, None]).astype(jnp.float32)

    def sequence_score(result):
        return jnp.sum(
            jnp.sum(result * readout_wide, axis=1).reshape(seqs_here, length) * living, axis=1
        )

    placed = jnp.zeros((2, all_seqs), jnp.float32)
    offset = data_rank * seqs_here
    placed = lax.dynamic_update_slice(
        placed,
        jnp.stack([sequence_score(ref_result), sequence_score(pol_result)]),
        (jnp.int32(0), offset),
    )
    scores = lax.psum(placed, ("dp", "tensor"))
    ratios = scores[1] - scores[0]
    chooser = (pairing[:, None] == jnp.arange(all_seqs)[None, :]).astype(jnp.float32)
    picked = jnp.dot(chooser, ratios, precision=lax.Precision.HIGHEST).reshape(-1, 2)
    margins = DPO_BETA * (picked[:, 0] - picked[:, 1])
    dpo_loss = jnp.sum(jax.nn.softplus(-margins))
    pair_pull = DPO_BETA * LOSS_SCALE * jax.nn.sigmoid(-margins)
    signed = jnp.stack([-pair_pull, pair_pull], axis=1).reshape(-1)
    coefficients = jnp.dot(signed, chooser, precision=lax.Precision.HIGHEST)
    local_coef = lax.dynamic_slice_in_dim(coefficients, offset, seqs_here)
    grad_result = (local_coef[:, None] * living).reshape(tok_rows, 1) * readout_wide
    (
        low_rank_update,
        query_rows,
        rotated_keys,
        value_rows,
        probs_low,
        probabilities,
        capped,
        summed,
        post_scale,
    ) = pol_saved
    post_dot = lax.psum(jnp.sum(summed * post_local * grad_result, axis=1), "tensor")
    grad_summed = (
        post_scale * post_local * grad_result
        - summed * post_scale**3 * post_dot[:, None] / full_width
    )
    grad_wide = lax.all_gather(grad_summed.astype(jnp.bfloat16), "tensor", axis=1, tiled=True)
    grad_mixed = jnp.dot(grad_wide, w_out_all, preferred_element_type=jnp.float32).astype(
        jnp.bfloat16
    )
    q_heads = query_rows.shape[2]
    grad_q_rot, rotated_key_gradient, value_head_gradient = attend_back(
        grad_mixed.reshape(seqs_here, length, q_heads, HEAD_SIZE),
        query_rows,
        rotated_keys,
        value_rows,
        probs_low,
        probabilities,
        capped,
    )
    query_rows_gradient = (
        apply_rotation(grad_q_rot, -1.0).reshape(tok_rows, -1).astype(jnp.bfloat16)
    )
    key_rows_gradient = (
        apply_rotation(rotated_key_gradient, -1.0).reshape(tok_rows, -1).astype(jnp.bfloat16)
    )
    value_rows_gradient = value_head_gradient.reshape(tok_rows, -1).astype(jnp.bfloat16)
    rank_size = query_second_factor.shape[0]
    rows_contraction = (((0,), (0,)), ((), ()))
    contract_cols = (((1,), (1,)), ((), ()))
    query_adapter_term = ADAPTER_SCALE * lax.dot_general(
        low_rank_update[:, :rank_size],
        query_rows_gradient,
        rows_contraction,
        preferred_element_type=jnp.float32,
    )
    value_adapter_term = ADAPTER_SCALE * lax.dot_general(
        low_rank_update[:, rank_size:],
        value_rows_gradient,
        rows_contraction,
        preferred_element_type=jnp.float32,
    )
    query_factor_gradient, value_factor_gradient = (
        lax.psum(query_adapter_term.astype(jnp.bfloat16), "dp").astype(jnp.float32),
        lax.psum(value_adapter_term.astype(jnp.bfloat16), "dp").astype(jnp.float32),
    )
    adapter_grad = jnp.concatenate(
        [
            ADAPTER_SCALE
            * lax.dot_general(
                query_rows_gradient,
                query_second_factor,
                contract_cols,
                preferred_element_type=jnp.float32,
            ),
            ADAPTER_SCALE
            * lax.dot_general(
                value_rows_gradient,
                value_second_factor,
                contract_cols,
                preferred_element_type=jnp.float32,
            ),
        ],
        axis=1,
    ).astype(jnp.bfloat16)
    adapter_term = lax.dot_general(
        pol_normed, adapter_grad, rows_contraction, preferred_element_type=jnp.float32
    )
    adapter_part = lax.psum_scatter(
        adapter_term.astype(jnp.bfloat16), "dp", scatter_dimension=0, tiled=True
    )
    grad_a = lax.psum(adapter_part, "tensor").astype(jnp.float32)
    a_both = jnp.concatenate([a_query_all, a_value_all], axis=1)
    input_terms = lax.dot_general(
        query_rows_gradient, w_query_all, contract_cols, preferred_element_type=jnp.float32
    )
    input_terms = input_terms + lax.dot_general(
        key_rows_gradient, w_key_all, contract_cols, preferred_element_type=jnp.float32
    )
    input_terms = input_terms + lax.dot_general(
        value_rows_gradient, w_value_all, contract_cols, preferred_element_type=jnp.float32
    )
    input_terms = input_terms + lax.dot_general(
        adapter_grad, a_both, contract_cols, preferred_element_type=jnp.float32
    )
    input_whole = lax.psum(input_terms.astype(jnp.bfloat16), "tensor").astype(jnp.float32)
    grad_normed = lax.dynamic_slice_in_dim(input_whole, tensor_rank * part_width, part_width, 1)
    narrow = pol_hidden.astype(jnp.float32)
    pre_dot = lax.psum(jnp.sum(narrow * pre_local * grad_normed, axis=1), "tensor")
    grad_hidden = (
        grad_result
        + pol_scale * pre_local * grad_normed
        - narrow * pol_scale**3 * pre_dot[:, None] / full_width
    )
    return (
        pol_result.astype(jnp.bfloat16),
        ref_result.astype(jnp.bfloat16),
        dpo_loss,
        grad_hidden.astype(jnp.bfloat16),
        grad_a,
        query_factor_gradient,
        value_factor_gradient,
    )


def solution(mesh):
    placed = (
        P("dp", "tensor"),
        P("dp", "tensor"),
        P("dp", "tensor"),
        P("dp"),
        P(),
        P(),
        P(),
        P("dp", "tensor"),
        P("dp", "tensor"),
        P("dp", "tensor"),
        P("dp", "tensor"),
        P("dp", None),
        P("dp", None),
        P(None, "tensor"),
        P(None, "tensor"),
    )
    return jax.shard_map(
        body,
        mesh=mesh,
        in_specs=placed,
        out_specs=(
            P("dp", "tensor"),
            P("dp", "tensor"),
            P(),
            P("dp", "tensor"),
            P("dp", None),
            P(None, "tensor"),
            P(None, "tensor"),
        ),
        check_vma=False,
    )
```

profile of v0, /device:TPU:0, one launch (start us, length us, event | category | flops | bytes accessed | tf_op | source)
XLA Modules:
  0.0 823.5 jit_solution(8016594998505936199)
XLA Ops:
  11.2 9.0 %all_gather.29 = bf16[4608,64]{0,1:T(8,128)(2,1)S(1)} all-gather(bf16[1152,64]{0,1:T(8,128)(2,1)S(1)} %copy-done.29), channel_id=1, replica_groups=mesh['dp'=4,'tensor'=8] {'dp'}, dimensions={0}, use_global_device_ids=true | all-gather | bytes 737280 | tf_op jit(solution)/shard_map/all_gather | solution.py:194
  20.3 7.6 all_gather.30
  29.8 41.2 %all-gather.21.cloned.1.call-done = bf16[8,576,288]{1,2,0:T(8,128)(2,1)} async-done(((bf16[1,576,288]{1,2,0:T(8,128)(2,1)}), bf16[8,576,288]{1,2,0:T(8,128)(2,1)}) %all-gather.21.cloned.1.call-update) | async-done | bytes 2654224 | tf_op jit(solution)/shard_map/all_gather | solution.py:95
  71.0 5.3 copy.72
  76.4 7.2 reshape.270
  83.6 46.3 %all-gather.19.cloned.1.call-done = bf16[8,576,288]{1,2,0:T(8,128)(2,1)} async-done(((bf16[1,576,288]{1,2,0:T(8,128)(2,1)}), bf16[8,576,288]{1,2,0:T(8,128)(2,1)}) %all-gather.19.cloned.1.call-update) | async-done | bytes 2654224 | tf_op jit(solution)/shard_map/all_gather | solution.py:95
  129.8 5.3 copy.64
  135.2 7.8 reshape.269
  143.0 3.1 multiply_reduce_fusion
  148.1 1.5 copy-done.1
  149.6 3.3 multiply_convert_fusion
  152.9 1.2 all-gather.13.cloned.1.call-done
  154.1 3.3 fusion.141
  157.6 3.2 fusion.139
  160.8 1.1 reshape.255
  162.0 17.6 %all-gather.11.cloned.1.call-done = bf16[4608,256]{1,0:T(8,128)(2,1)} async-done(((bf16[1152,256]{1,0:T(8,128)(2,1)}), bf16[4608,256]{1,0:T(8,128)(2,1)}) %all-gather.11.cloned.1.call-update) | async-done | bytes 2359312 | tf_op jit(solution)/shard_map/all_gather | solution.py:192
  179.6 3.3 convolution_convert_fusion.6
  186.1 32.4 %all-gather.15.cloned.1.call-done = bf16[4608,512]{1,0:T(8,128)(2,1)} async-done(((bf16[1152,512]{1,0:T(8,128)(2,1)}), bf16[4608,512]{1,0:T(8,128)(2,1)}) %all-gather.15.cloned.1.call-update) | async-done | bytes 4718608 | tf_op jit(solution)/shard_map/all_gather | solution.py:190
  218.5 5.5 fusion.142
  224.0 1.3 reshape.258
  225.2 4.4 fusion.140
  229.6 1.0 fusion.2
  230.7 2.1 reshape.256
  232.8 2.9 subtract_convert_fusion.1
  235.8 1.3 fusion.12
  237.1 1.5 fusion.15
  239.0 18.4 %all-gather.17.cloned.1.call-done = bf16[4608,512]{1,0:T(8,128)(2,1)} async-done(((bf16[1152,512]{1,0:T(8,128)(2,1)}), bf16[4608,512]{1,0:T(8,128)(2,1)}) %all-gather.17.cloned.1.call-update) | async-done | bytes 4718608 | tf_op jit(solution)/shard_map/all_gather | solution.py:193
  257.4 5.4 convolution_convert_fusion
  262.8 4.7 copy.110
  267.8 2.5 fusion.138
  272.4 1.6 fusion.54
  276.2 5.6 convolution_convert_fusion.1
  281.8 4.7 copy.108
  288.0 59.2 %reduce-scatter.12.cloned.1.call-done = bf16[576,288]{1,0:T(8,128)(2,1)} async-done(((bf16[4608,288]{1,0:T(8,128)(2,1)}), bf16[576,288]{1,0:T(8,128)(2,1)}) %reduce-scatter.12.cloned.1.call-update) | async-done | bytes 331792
  347.1 1.9 copy.111
  349.1 80.8 %reduce-scatter.10.cloned.1.call-done = bf16[576,288]{1,0:T(8,128)(2,1)} async-done(((bf16[4608,288]{1,0:T(8,128)(2,1)}), bf16[576,288]{1,0:T(8,128)(2,1)}) %reduce-scatter.10.cloned.1.call-update) | async-done | bytes 331792
  429.8 1.2 copy.109
  431.2 1.2 fusion.32
  432.4 20.1 %all-reduce = (f32[288]{0:T(512)S(1)}, f32[288]{0:T(512)S(1)}) all-reduce(f32[288]{0:T(512)S(1)} %fusion.45, f32[288]{0:T(512)S(1)} %fusion.32), channel_id=1, replica_groups=mesh['dp'=4,'tensor'=8] {'tensor'}, use_global_device_ids=true, to_apply=%region_4.5 | all-reduce | flops 576 | bytes 4608 | tf_op jit(solution)/shard_map/psum | solution.py:146
  452.5 2.6 fusion.43
  457.0 36.8 %psum.65 = f32[2,12]{1,0:T(2,128)S(1)} all-reduce(f32[2,12]{1,0:T(2,128)S(1)} %dynamic_update_slice.3), channel_id=1, replica_groups=mesh['dp'=4,'tensor'=8] {'dp','tensor'}, use_global_device_ids=true, to_apply=%region_14.15 | all-reduce | flops 24 | bytes 192 | tf_op jit(solution)/shard_map/psum | solution.py:226
  496.8 21.1 %psum.66 = f32[288]{0:T(512)S(1)} all-reduce(f32[288]{0:T(512)S(1)} %fusion.38), channel_id=1, replica_groups=mesh['dp'=4,'tensor'=8] {'tensor'}, use_global_device_ids=true, to_apply=%region_17.18 | all-reduce | flops 288 | bytes 2304 | tf_op jit(solution)/shard_map/psum | solution.py:248
  517.9 1.1 fusion.55
  519.2 55.1 %all-gather.23.cloned.1.call-done = bf16[8,576,288]{1,2,0:T(8,128)(2,1)} async-done(((bf16[1,576,288]{1,2,0:T(8,128)(2,1)}), bf16[8,576,288]{1,2,0:T(8,128)(2,1)}) %all-gather.23.cloned.1.call-update) | async-done | bytes 2654224 | tf_op jit(solution)/shard_map/all_gather | solution.py:253
  574.4 4.4 copy.82
  578.8 5.6 reshape.268
  584.4 5.4 convolution_convert_fusion.3
  590.9 2.1 convolution_bitcast_fusion
  592.9 2.0 fusion.19
  595.0 3.3 fusion.27
  598.3 1.5 fusion.135
  602.9 2.2 convolution_convert_fusion.2
  605.2 2.5 convolution_bitcast_fusion.2
  609.0 4.3 fusion.58
  616.3 2.4 fusion.1
  618.7 10.8 %reduce-scatter.8.cloned.1.call-done = bf16[1152,128]{1,0:T(8,128)(2,1)} async-done(((bf16[4608,128]{1,0:T(8,128)(2,1)}), bf16[1152,128]{1,0:T(8,128)(2,1)}) %reduce-scatter.8.cloned.1.call-update) | async-done | bytes 294928 | tf_op jit(solution)/shard_map/reduce_scatter | solution.py:315
  631.2 10.5 %psum.71 = bf16[64,256]{1,0:T(8,128)(2,1)S(1)} all-reduce(bf16[64,256]{1,0:T(8,128)(2,1)S(1)} %fusion.23), channel_id=1, replica_groups=mesh['dp'=4,'tensor'=8] {'dp'}, use_global_device_ids=true, to_apply=%region_25.26 | all-reduce | flops 16384 | bytes 65536 | tf_op jit(solution)/shard_map/psum | solution.py:291
  642.4 21.6 %all-reduce.5.cloned.1.call-done = bf16[64,512]{1,0:T(8,128)(2,1)} async-done(((bf16[64,512]{1,0:T(8,128)(2,1)}), bf16[64,512]{1,0:T(8,128)(2,1)}) %all-reduce.5.cloned.1.call-update) | async-done | bytes 65552 | tf_op jit(solution)/shard_map/psum | solution.py:290
  664.0 1.5 convert_element_type.173
  665.5 126.0 %all-reduce.7.cloned.1.call-done = (bf16[288,4608]{1,0:T(8,128)(2,1)}, bf16[1152,128]{1,0:T(8,128)(2,1)}) async-done(((bf16[288,4608]{1,0:T(8,128)(2,1)}, bf16[1152,128]{1,0:T(8,128)(2,1)}), (bf16[288,4608]{1,0:T(8,128)(2,1)}, bf16[1152,128]{1,0:T(8,128)(2,1)})) %all-reduce.7.cloned.1.call-update) | async-done | bytes 2949136 | tf_op jit(solution)/shard_map/psum | solution.py:332
  791.5 1.3 fusion.35
  792.8 19.4 %psum.68 = f32[288]{0:T(512)S(1)} all-reduce(f32[288]{0:T(512)S(1)} %fusion.35), channel_id=1, replica_groups=mesh['dp'=4,'tensor'=8] {'tensor'}, use_global_device_ids=true, to_apply=%region_21.22 | all-reduce | flops 288 | bytes 2304 | tf_op jit(solution)/shard_map/psum | solution.py:335
  812.3 1.8 convert_element_type.171
  814.1 2.4 fusion.40
  (179 shorter events, 33.4 us)
Async XLA Ops:
  7.2 222.5 %copy-start = (bf16[64,512]{1,0:T(8,128)(2,1)S(1)}, bf16[64,512]{1,0:T(8,128)(2,1)}, u32[]{:S(2)}) copy-start(bf16[64,512]{1,0:T(8,128)(2,1)} %param.28) | copy-start | bytes 196612
  7.2 4.1 copy-start.29
  7.2 63.8 %all-gather.21.cloned.1.call-start = ((), (), s32[]{:S(2)}) async-start(), calls=%async_computation.10 | async-start | bytes 3317760 | tf_op jit(solution)/shard_map/all_gather | solution.py:95
  7.9 121.9 %all-gather.19.cloned.1.call-start = ((), (), s32[]{:S(2)}) async-start(), calls=%async_computation.9 | async-start | bytes 3317760 | tf_op jit(solution)/shard_map/all_gather | solution.py:95
  8.7 11.6 %copy-start.30 = (bf16[1152,64]{0,1:T(8,128)(2,1)S(1)}, bf16[1152,64]{0,1:T(8,128)(2,1)}, u32[]{:S(2)}) copy-start(bf16[1152,64]{0,1:T(8,128)(2,1)} %param.27) | copy-start | bytes 442372
  8.7 145.4 %all-gather.13.cloned.1.call-start = ((), (), s32[]{:S(2)}) async-start(), calls=%async_computation.4 | async-start | bytes 2949120 | tf_op jit(solution)/shard_map/all_gather | solution.py:191
  9.4 170.2 %all-gather.11.cloned.1.call-start = ((), (), s32[]{:S(2)}) async-start(), calls=%async_computation.3 | async-start | bytes 2949120 | tf_op jit(solution)/shard_map/all_gather | solution.py:192
  10.0 18.0 %copy-start.40 = (s32[3]{0:T(128)S(1)}, s32[3]{0:T(128)}, u32[]{:S(2)}) copy-start(s32[3]{0:T(128)} %param.18) | copy-start | bytes 40
  10.0 208.5 %all-gather.15.cloned.1.call-start = ((), (), s32[]{:S(2)}) async-start(), calls=%async_computation.5 | async-start | bytes 5898240 | tf_op jit(solution)/shard_map/all_gather | solution.py:190
  10.6 246.8 %all-gather.17.cloned.1.call-start = ((), (), s32[]{:S(2)}) async-start(), calls=%async_computation.6 | async-start | bytes 5898240 | tf_op jit(solution)/shard_map/all_gather | solution.py:193
  11.2 336.0 %reduce-scatter.12.cloned.1.call-start = ((), (), s32[]{:S(2)}) async-start(), calls=%async_computation.13 | async-start | bytes 3981312
  28.1 48.3 %copy-start.3 = (bf16[4608,128]{0,1:T(8,128)(2,1)}, bf16[4608,128]{0,1:T(8,128)(2,1)S(1)}, u32[]{:S(2)}) copy-start(bf16[4608,128]{0,1:T(8,128)(2,1)S(1)} %constant_dynamic-update-slice_fusion) | copy-start | bytes 3538948
  29.8 203.0 %copy-start.12 = (f32[96,64]{1,0:T(8,128)}, f32[96,64]{1,0:T(8,128)S(1)}, u32[]{:S(2)}) copy-start(f32[96,64]{1,0:T(8,128)S(1)} %get-tuple-element.50) | copy-start | bytes 73732
  135.2 12.9 %copy-start.36 = (f32[4608]{0:T(1024)S(1)}, f32[4608]{0:T(1024)}, u32[]{:S(2)}) copy-start(f32[4608]{0:T(1024)} %param.20) | copy-start | bytes 55300
  143.0 4.1 copy-start.2
  147.1 2.5 copy-start.1
  148.1 4.9 copy-start.37
  183.6 1.6 copy-start.4
  232.7 3.0 copy-start.25
  232.7 3.0 copy-start.26
  232.8 3.0 copy-start.31
  235.7 1.4 copy-start.27
  267.6 2.8 copy-start.34
  267.6 4.6 copy-start.15
  267.6 4.7 copy-start.14
  267.6 162.2 %reduce-scatter.10.cloned.1.call-start = ((), (), s32[]{:S(2)}) async-start(), calls=%async_computation.12 | async-start | bytes 3981312
  272.2 2.9 copy-start.16
  272.2 2.6 copy-start.32
  272.3 1.7 copy-start.19
  272.3 3.9 copy-start.20
  274.0 0.8 copy-start.43
  274.0 0.8 copy-start.44
  286.5 0.7 copy-start.41
  286.5 166.0 %copy-start.6 = (bf16[288,576]{1,0:T(8,128)(2,1)S(1)}, bf16[288,576]{1,0:T(8,128)(2,1)}, u32[]{:S(2)}) copy-start(bf16[288,576]{1,0:T(8,128)(2,1)} %param.17) | copy-start | bytes 995332
  286.5 287.9 %all-gather.23.cloned.1.call-start = ((), (), s32[]{:S(2)}) async-start(), calls=%async_computation.11 | async-start | bytes 3317760 | tf_op jit(solution)/shard_map/all_gather | solution.py:253
  519.0 110.6 %reduce-scatter.8.cloned.1.call-start = ((), (), s32[]{:S(2)}) async-start(), calls=%async_computation.7 | async-start | bytes 1474560 | tf_op jit(solution)/shard_map/reduce_scatter | solution.py:315
  584.4 8.5 %copy-start.33 = (pred[3,96,96]{1,2,0:T(8,128)(4,1)S(1)}, pred[3,96,96]{1,2,0:T(8,128)(4,1)}, u32[]{:S(2)}) copy-start(pred[3,96,96]{1,2,0:T(8,128)(4,1)} %broadcast_and_fusion) | copy-start | bytes 82948
  584.4 8.5 %copy-start.45 = (f32[3,2,2,96]{3,2,1,0:T(2,128)S(1)}, f32[3,2,2,96]{3,2,1,0:T(2,128)}, u32[]{:S(2)}) copy-start(f32[3,2,2,96]{3,2,1,0:T(2,128)} %copy-done.44) | copy-start | bytes 13828
  595.0 4.8 copy-start.28
  595.0 5.6 copy-start.35
  595.0 5.8 copy-start.13
  595.0 5.8 copy-start.17
  599.9 0.7 copy-start.10
  600.8 1.5 copy-start.21
  602.3 0.6 copy-start.23
  605.1 2.6 copy-start.18
  605.1 58.9 %all-reduce.5.cloned.1.call-start = ((), (), s32[]{:S(2)}) async-start(), calls=%async_computation.8 | async-start | bytes 131072 | tf_op jit(solution)/shard_map/psum | solution.py:290
  609.0 4.3 copy-start.8
  609.0 182.5 %all-reduce.7.cloned.1.call-start = ((), (), s32[]{:S(2)}) async-start(), calls=%async_computation.14 | async-start | bytes 5898240 | tf_op jit(solution)/shard_map/psum | solution.py:332
  613.3 1.7 copy-start.9
  613.3 1.7 copy-start.11
  615.0 1.3 copy-start.5
  615.0 1.3 copy-start.22
  615.0 1.3 copy-start.24
  618.7 11.6 %copy-start.42 = (f32[6,1]{0,1:T(1,128)S(1)}, f32[6,1]{0,1:T(1,128)}, u32[]{:S(2)}) copy-start(f32[6,1]{0,1:T(1,128)} %get-tuple-element.17) | copy-start | bytes 76
  618.7 172.8 %copy-start.7 = (bf16[288,576]{1,0:T(8,128)(2,1)S(1)}, bf16[288,576]{1,0:T(8,128)(2,1)}, u32[]{:S(2)}) copy-start(bf16[288,576]{1,0:T(8,128)(2,1)} %param.16) | copy-start | bytes 995332
  618.7 195.4 %copy-start.38 = (f32[288]{0:T(512)S(1)}, f32[288]{0:T(512)}, u32[]{:S(2)}) copy-start(f32[288]{0:T(512)} %copy-done.37) | copy-start | bytes 3460
  618.7 195.4 %copy-start.39 = (f32[288]{0:T(512)S(1)}, f32[288]{0:T(512)}, u32[]{:S(2)}) copy-start(f32[288]{0:T(512)} %get-tuple-element.44) | copy-start | bytes 3460
Sparse Core Ops, SparseCore 0:
  10.2 60.8 all-gather.20
  73.2 56.5 all-gather.18
  131.4 22.6 all-gather.12
  155.5 24.0 all-gather.10
  181.0 37.4 all-gather.14
  219.9 37.4 all-gather.16
  267.7 79.4 reduce-scatter.11
  350.8 79.0 reduce-scatter.9
  519.1 55.2 all-gather.22
  605.2 24.2 reduce-scatter.7
  632.4 31.5 all-reduce.4
  667.5 123.9 all-reduce.6
where the time goes:
time: 829 us; the launch traced here: 824 us
  waiting for transfers between devices  514 us (62%)
  blocking collectives  125 us (15%)
  matrix products  69.4 us (8%)
  local copies, waits for them, and re-layouts  68.9 us (8%)
  other arithmetic  30.4 us (4%)
  between operations  15.1 us (2%)
    unnamed x14, waiting for transfers between devices  144 us
    psum x1, waiting for transfers between devices, body(): lax.psum(input_terms.astype(jnp.bfloat16), 'tensor').astype(jnp.float32)  126 us
    all_gather x2, waiting for transfers between devices, normalize(): whole_rows = lax.all_gather(hidden, 'tensor', axis=1, tiled=True)  87.5 us
    all_gather x1, waiting for transfers between devices, body(): lax.all_gather(grad_summed.astype(jnp.bfloat16), 'tensor', axis=1, tiled=...  55.1 us
    psum x1, blocking collectives, body(): scores = lax.psum(placed, ('dp', 'tensor'))  36.8 us
    all_gather x1, waiting for transfers between devices, body(): lax.all_gather(w_query, 'dp', axis=0, tiled=True)  32.4 us
    convert_element_type x4, local copies, waits for them, and re-layouts, normalize(): wide_rows = whole_rows.astype(jnp.float32)  25.6 us
    unnamed x98, local copies, waits for them, and re-layouts  24.7 us
  transfers between devices with their start and end apart: 12, of which 12 were waited for; matrix products, arithmetic and copies ran while one was open for 13% of the time, Pallas kernels for 0%

commit v1 on v0

--- a/solution.py
+++ b/solution.py
@@ -92,7 +92,14 @@
 
 
 def normalize(hidden, pre_gain):
-    whole_rows = lax.all_gather(hidden, "tensor", axis=1, tiled=True)
+    size = lax.axis_size("tensor")
+    forward = [(i, (i + 1) % size) for i in range(size)]
+    blocks = [hidden]
+    for far in range(1, size):
+        blocks = [lax.ppermute(blocks[0], "tensor", forward), *blocks]
+    out = jnp.concatenate(blocks, axis=1)
+    shift = (lax.axis_index("tensor") + 1) * blocks[-1].shape[1]
+    whole_rows = jnp.roll(out, shift, axis=1)
     wide_rows = whole_rows.astype(jnp.float32)
     pre_scale = lax.rsqrt(
         jnp.sum(wide_rows * wide_rows, axis=1, keepdims=True) / pre_gain.shape[0] + NORM_EPS

time: 829 us -> 751 us (0.906)
  waiting for transfers between devices: 514 us -> 439 us
  local copies, waits for them, and re-layouts: 68.9 us -> 52.3 us
    all_gather x2 -> x0, waiting for transfers between devices: 87.5 us -> none  [normalize(): whole_rows = lax.all_gather(hidden, 'tensor', axis=1, tiled=True)]
    ppermute x0 -> x14, waiting for transfers between devices: none -> 86.5 us  [normalize(): blocks = [lax.ppermute(blocks[0], 'tensor', forward), *blocks]]
    all_gather x1, waiting for transfers between devices: 32.4 us -> 0.01 us  [body(): lax.all_gather(w_query, 'dp', axis=0, tiled=True)]
    convert_element_type x4 -> x0, local copies, waits for them, and re-layouts: 25.6 us -> none  [normalize(): wide_rows = whole_rows.astype(jnp.float32)]
    all_gather x1, waiting for transfers between devices: 18.4 us -> 0.01 us  [body(): lax.all_gather(w_out, 'dp', axis=0, tiled=True)]
    all_gather x1, waiting for transfers between devices: 17.6 us -> 0.02 us  [body(): lax.all_gather(value_projection, 'dp', axis=0, tiled=True)]
    concatenate x0 -> x2, local copies, waits for them, and re-layouts: none -> 9.44 us  [normalize(): out = jnp.concatenate(blocks, axis=1)]
    unnamed x14 -> x12, waiting for transfers between devices: 144 us -> 139 us
  transfers between devices with their start and end apart: 12 -> 24, of which waited for: 12 -> 19; matrix products, arithmetic and copies ran while one was open for 13% -> 14% of each run, Pallas kernels for 0% -> 0%
where the time goes in v1:
time: 751 us; the launch traced here: 746 us
  waiting for transfers between devices  439 us (58%)
  blocking collectives  127 us (17%)
  matrix products  72 us (10%)
  local copies, waits for them, and re-layouts  52.3 us (7%)
  other arithmetic  34 us (5%)
  between operations  15.2 us (2%)
    unnamed x12, waiting for transfers between devices  139 us
    psum x1, waiting for transfers between devices, body(): lax.psum(input_terms.astype(jnp.bfloat16), 'tensor').astype(jnp.float32)  126 us
    ppermute x14, waiting for transfers between devices, normalize(): blocks = [lax.ppermute(blocks[0], 'tensor', forward), *blocks]  86.5 us
    all_gather x1, waiting for transfers between devices, body(): lax.all_gather(grad_summed.astype(jnp.bfloat16), 'tensor', axis=1, tiled=...  55.1 us
    psum x1, blocking collectives, body(): scores = lax.psum(placed, ('dp', 'tensor'))  36.8 us
    unnamed x116, local copies, waits for them, and re-layouts  22.9 us
    psum x1, waiting for transfers between devices, body(): lax.psum(query_adapter_term.astype(jnp.bfloat16), 'dp').astype(jnp.float32)  21.6 us
    psum x1, blocking collectives, body(): lax.psum(jnp.sum(summed * post_local * grad_result, axis=1), 'tensor')  21.1 us
  transfers between devices with their start and end apart: 24, of which 19 were waited for; matrix products, arithmetic and copies ran while one was open for 14% of the time, Pallas kernels for 0%

profile of v1, /device:TPU:0, one launch (start us, length us, event | category | flops | bytes accessed | tf_op | source)
XLA Modules:
  0.0 745.9 jit_solution(11917479473526976985)
XLA Ops:
  9.5 3.0 collective-permute-start.7
  12.5 1.5 collective-permute-start
  14.1 11.1 %collective-permute-done.7 = bf16[288,576]{1,0:T(8,128)(2,1)S(1)} collective-permute-done((bf16[288,576]{1,0:T(8,128)(2,1)}, bf16[288,576]{1,0:T(8,128)(2,1)S(1)}, u32[]{:S(2)}, u32[]{:S(2)}) %collective-permute-start.7) | collective-permute-done | bytes 331808 | tf_op jit(solution)/shard_map/ppermute | solution.py:99
  25.2 7.9 %collective-permute-done = bf16[288,576]{1,0:T(8,128)(2,1)S(1)} collective-permute-done((bf16[288,576]{1,0:T(8,128)(2,1)}, bf16[288,576]{1,0:T(8,128)(2,1)S(1)}, u32[]{:S(2)}, u32[]{:S(2)}) %collective-permute-start) | collective-permute-done | bytes 331808 | tf_op jit(solution)/shard_map/ppermute | solution.py:99
  33.9 7.1 collective-permute-done.8
  41.0 7.9 %collective-permute-done.1 = bf16[288,576]{1,0:T(8,128)(2,1)S(1)} collective-permute-done((bf16[288,576]{1,0:T(8,128)(2,1)S(1)}, bf16[288,576]{1,0:T(8,128)(2,1)S(1)}, u32[]{:S(2)}, u32[]{:S(2)}) %collective-permute-start.1) | collective-permute-done | bytes 331808 | tf_op jit(solution)/shard_map/ppermute | solution.py:99
  49.0 11.3 %all_gather.22 = bf16[4608,64]{0,1:T(8,128)(2,1)S(1)} all-gather(bf16[1152,64]{0,1:T(8,128)(2,1)S(1)} %copy-done.41), channel_id=1, replica_groups=mesh['dp'=4,'tensor'=8] {'dp'}, dimensions={0}, use_global_device_ids=true | all-gather | bytes 737280 | tf_op jit(solution)/shard_map/all_gather | solution.py:201
  61.6 2.2 collective-permute-done.2
  64.8 7.5 %all_gather.23 = bf16[4608,64]{0,1:T(8,128)(2,1)S(1)} all-gather(bf16[1152,64]{0,1:T(8,128)(2,1)S(1)} %copy-done.42), channel_id=1, replica_groups=mesh['dp'=4,'tensor'=8] {'dp'}, dimensions={0}, use_global_device_ids=true | all-gather | bytes 737280 | tf_op jit(solution)/shard_map/all_gather | solution.py:202
  72.3 2.1 collective-permute-done.10
  74.4 7.9 %collective-permute-done.3 = bf16[288,576]{1,0:T(8,128)(2,1)S(1)} collective-permute-done((bf16[288,576]{1,0:T(8,128)(2,1)S(1)}, bf16[288,576]{1,0:T(8,128)(2,1)S(1)}, u32[]{:S(2)}, u32[]{:S(2)}) %collective-permute-start.3) | collective-permute-done | bytes 331808 | tf_op jit(solution)/shard_map/ppermute | solution.py:99
  83.4 6.9 collective-permute-done.11
  90.2 7.9 %collective-permute-done.4 = bf16[288,576]{1,0:T(8,128)(2,1)S(1)} collective-permute-done((bf16[288,576]{1,0:T(8,128)(2,1)S(1)}, bf16[288,576]{1,0:T(8,128)(2,1)S(1)}, u32[]{:S(2)}, u32[]{:S(2)}) %collective-permute-start.4) | collective-permute-done | bytes 331808 | tf_op jit(solution)/shard_map/ppermute | solution.py:99
  98.9 7.1 collective-permute-done.12
  106.0 8.0 %collective-permute-done.5 = bf16[288,576]{1,0:T(8,128)(2,1)} collective-permute-done((bf16[288,576]{1,0:T(8,128)(2,1)S(1)}, bf16[288,576]{1,0:T(8,128)(2,1)}, u32[]{:S(2)}, u32[]{:S(2)}) %collective-permute-start.5) | collective-permute-done | bytes 331808 | tf_op jit(solution)/shard_map/ppermute | solution.py:99
  115.3 6.7 collective-permute-done.13
  122.0 3.9 concatenate.57
  125.9 3.6 collective-permute-done.6
  129.5 5.5 concatenate.51
  135.0 2.8 fusion.5
  137.9 2.7 fusion.2
  141.2 7.0 fusion.7
  148.2 2.1 convolution_convert_fusion.7
  152.3 3.3 fusion.145
  155.8 3.2 fusion.144
  160.2 3.2 fusion.23
  166.0 5.5 fusion.146
  172.7 4.8 convolution_add_fusion.3
  177.5 2.1 reshape.256
  179.6 2.9 subtract_convert_fusion.1
  185.4 5.5 convolution_convert_fusion.1
  190.9 4.8 copy.104
  196.0 4.0 convolution_convert_fusion.6
  200.0 1.6 convert_element_type.151
  201.7 2.2 fusion.19
  203.9 1.6 fusion.22
  205.9 5.5 convolution_convert_fusion
  211.4 4.7 copy.106
  217.6 56.1 %reduce-scatter.10.cloned.1.call-done = bf16[576,288]{1,0:T(8,128)(2,1)} async-done(((bf16[4608,288]{1,0:T(8,128)(2,1)}), bf16[576,288]{1,0:T(8,128)(2,1)}) %reduce-scatter.10.cloned.1.call-update) | async-done | bytes 331792
  275.1 81.2 %reduce-scatter.12.cloned.1.call-done = bf16[576,288]{1,0:T(8,128)(2,1)} async-done(((bf16[4608,288]{1,0:T(8,128)(2,1)}), bf16[576,288]{1,0:T(8,128)(2,1)}) %reduce-scatter.12.cloned.1.call-update) | async-done | bytes 331792
  356.3 1.9 copy.107
  359.4 20.0 %all-reduce = (f32[288]{0:T(512)S(1)}, f32[288]{0:T(512)S(1)}) all-reduce(f32[288]{0:T(512)S(1)} %fusion.51, f32[288]{0:T(512)S(1)} %fusion.38), channel_id=1, replica_groups=mesh['dp'=4,'tensor'=8] {'tensor'}, use_global_device_ids=true, to_apply=%region_4.6 | all-reduce | flops 576 | bytes 4608 | tf_op jit(solution)/shard_map/psum | solution.py:153
  379.4 2.6 fusion.49
  382.7 36.8 %psum.65 = f32[2,12]{1,0:T(2,128)S(1)} all-reduce(f32[2,12]{1,0:T(2,128)S(1)} %dynamic_update_slice.3), channel_id=1, replica_groups=mesh['dp'=4,'tensor'=8] {'dp','tensor'}, use_global_device_ids=true, to_apply=%region_14.16 | all-reduce | flops 24 | bytes 192 | tf_op jit(solution)/shard_map/psum | solution.py:233
  420.7 21.1 %psum.66 = f32[288]{0:T(512)S(1)} all-reduce(f32[288]{0:T(512)S(1)} %fusion.44), channel_id=1, replica_groups=mesh['dp'=4,'tensor'=8] {'tensor'}, use_global_device_ids=true, to_apply=%region_17.19 | all-reduce | flops 288 | bytes 2304 | tf_op jit(solution)/shard_map/psum | solution.py:255
  443.1 55.1 %all-gather.15.cloned.1.call-done = bf16[8,576,288]{1,2,0:T(8,128)(2,1)} async-done(((bf16[1,576,288]{1,2,0:T(8,128)(2,1)}), bf16[8,576,288]{1,2,0:T(8,128)(2,1)}) %all-gather.15.cloned.1.call-update) | async-done | bytes 2654224 | tf_op jit(solution)/shard_map/all_gather | solution.py:260
  498.3 4.4 copy.78
  502.7 5.6 reshape.264
  508.3 5.4 convolution_convert_fusion.3
  514.8 1.4 fusion.25
  518.3 3.3 fusion.33
  521.6 1.5 fusion.141
  525.2 2.2 convolution_convert_fusion.2
  527.5 2.5 convolution_bitcast_fusion.2
  531.4 4.3 fusion.64
  538.3 3.7 fusion.1
  542.0 9.9 %reduce-scatter.8.cloned.1.call-done = bf16[1152,128]{1,0:T(8,128)(2,1)} async-done(((bf16[4608,128]{1,0:T(8,128)(2,1)}), bf16[1152,128]{1,0:T(8,128)(2,1)}) %reduce-scatter.8.cloned.1.call-update) | async-done | bytes 294928 | tf_op jit(solution)/shard_map/reduce_scatter | solution.py:322
  553.6 10.5 %psum.71 = bf16[64,256]{1,0:T(8,128)(2,1)S(1)} all-reduce(bf16[64,256]{1,0:T(8,128)(2,1)S(1)} %fusion.29), channel_id=1, replica_groups=mesh['dp'=4,'tensor'=8] {'dp'}, use_global_device_ids=true, to_apply=%region_25.27 | all-reduce | flops 16384 | bytes 65536 | tf_op jit(solution)/shard_map/psum | solution.py:298
  564.8 21.6 %all-reduce.5.cloned.1.call-done = bf16[64,512]{1,0:T(8,128)(2,1)} async-done(((bf16[64,512]{1,0:T(8,128)(2,1)}), bf16[64,512]{1,0:T(8,128)(2,1)}) %all-reduce.5.cloned.1.call-update) | async-done | bytes 65552 | tf_op jit(solution)/shard_map/psum | solution.py:297
  586.4 1.5 convert_element_type.173
  587.9 126.0 %all-reduce.7.cloned.1.call-done = (bf16[288,4608]{1,0:T(8,128)(2,1)}, bf16[1152,128]{1,0:T(8,128)(2,1)}) async-done(((bf16[288,4608]{1,0:T(8,128)(2,1)}, bf16[1152,128]{1,0:T(8,128)(2,1)}), (bf16[288,4608]{1,0:T(8,128)(2,1)}, bf16[1152,128]{1,0:T(8,128)(2,1)})) %all-reduce.7.cloned.1.call-update) | async-done | bytes 2949136 | tf_op jit(solution)/shard_map/psum | solution.py:339
  715.3 19.4 %psum.68 = f32[288]{0:T(512)S(1)} all-reduce(f32[288]{0:T(512)S(1)} %fusion.41), channel_id=1, replica_groups=mesh['dp'=4,'tensor'=8] {'tensor'}, use_global_device_ids=true, to_apply=%region_21.23 | all-reduce | flops 288 | bytes 2304 | tf_op jit(solution)/shard_map/psum | solution.py:342
  734.7 1.8 convert_element_type.171
  736.5 2.4 fusion.46
  (217 shorter events, 39.6 us)
Async XLA Ops:
  7.2 144.1 %copy-start = (bf16[64,512]{1,0:T(8,128)(2,1)S(1)}, bf16[64,512]{1,0:T(8,128)(2,1)}, u32[]{:S(2)}) copy-start(bf16[64,512]{1,0:T(8,128)(2,1)} %param.30) | copy-start | bytes 196612
  7.2 41.8 %copy-start.41 = (bf16[1152,64]{0,1:T(8,128)(2,1)S(1)}, bf16[1152,64]{0,1:T(8,128)(2,1)}, u32[]{:S(2)}) copy-start(bf16[1152,64]{0,1:T(8,128)(2,1)} %param.28) | copy-start | bytes 442372
  7.2 57.6 %copy-start.42 = (bf16[1152,64]{0,1:T(8,128)(2,1)S(1)}, bf16[1152,64]{0,1:T(8,128)(2,1)}, u32[]{:S(2)}) copy-start(bf16[1152,64]{0,1:T(8,128)(2,1)} %param.29) | copy-start | bytes 442372
  7.2 145.1 %all-gather.9.cloned.1.call-start = ((), (), s32[]{:S(2)}) async-start(), calls=%async_computation.4 | async-start | bytes 2949120 | tf_op jit(solution)/shard_map/all_gather | solution.py:198
  7.9 152.2 %all-gather.7.cloned.1.call-start = ((), (), s32[]{:S(2)}) async-start(), calls=%async_computation.3 | async-start | bytes 2949120 | tf_op jit(solution)/shard_map/all_gather | solution.py:199
  8.7 157.3 %all-gather.11.cloned.1.call-start = ((), (), s32[]{:S(2)}) async-start(), calls=%async_computation.5 | async-start | bytes 5898240 | tf_op jit(solution)/shard_map/all_gather | solution.py:197
  9.4 73.9 %copy-start.51 = (s32[3]{0:T(128)S(1)}, s32[3]{0:T(128)}, u32[]{:S(2)}) copy-start(s32[3]{0:T(128)} %param.20) | copy-start | bytes 40
  9.4 112.5 %copy-start.11 = (bf16[288,576]{1,0:T(8,128)(2,1)S(1)}, bf16[288,576]{1,0:T(8,128)(2,1)}, u32[]{:S(2)}) copy-start(bf16[288,576]{1,0:T(8,128)(2,1)} %param.17) | copy-start | bytes 995332
  9.4 176.0 %all-gather.13.cloned.1.call-start = ((), (), s32[]{:S(2)}) async-start(), calls=%async_computation.6 | async-start | bytes 5898240 | tf_op jit(solution)/shard_map/all_gather | solution.py:200
  9.5 15.7 %collective-permute-start.7 = (bf16[288,576]{1,0:T(8,128)(2,1)}, bf16[288,576]{1,0:T(8,128)(2,1)S(1)}, u32[]{:S(2)}, u32[]{:S(2)}) collective-permute-start(bf16[288,576]{1,0:T(8,128)(2,1)} %param.17), channel_id=1, source_target_pairs={{0,1},{1,2},{2,3},{3,4},{4,5},{5,6},{6,7},{7,0},{8,9},{9,10},{10,1... | collective-permute-start | bytes 995336 | tf_op jit(solution)/shard_map/ppermute | solution.py:99
  12.5 20.6 %collective-permute-start = (bf16[288,576]{1,0:T(8,128)(2,1)}, bf16[288,576]{1,0:T(8,128)(2,1)S(1)}, u32[]{:S(2)}, u32[]{:S(2)}) collective-permute-start(bf16[288,576]{1,0:T(8,128)(2,1)} %param.18), channel_id=1, source_target_pairs={{0,1},{1,2},{2,3},{3,4},{4,5},{5,6},{6,7},{7,0},{8,9},{9,10},{10,1... | collective-permute-start | bytes 995336 | tf_op jit(solution)/shard_map/ppermute | solution.py:99
  25.2 23.7 %copy-start.22 = (bf16[288,576]{1,0:T(8,128)(2,1)}, bf16[288,576]{1,0:T(8,128)(2,1)S(1)}, u32[]{:S(2)}) copy-start(bf16[288,576]{1,0:T(8,128)(2,1)S(1)} %collective-permute-done.7) | copy-start | bytes 995332
  25.2 15.8 %collective-permute-start.8 = (bf16[288,576]{1,0:T(8,128)(2,1)S(1)}, bf16[288,576]{1,0:T(8,128)(2,1)S(1)}, u32[]{:S(2)}, u32[]{:S(2)}) collective-permute-start(bf16[288,576]{1,0:T(8,128)(2,1)S(1)} %collective-permute-done.7), channel_id=1, source_target_pairs={{0,1},{1,2},{2,3},{3,4},{4,5},{5,6},{6,7},{7,0},{8,9},{9,10},{10,1... | collective-permute-start | bytes 995336 | tf_op jit(solution)/shard_map/ppermute | solution.py:99
  33.8 15.1 %collective-permute-start.1 = (bf16[288,576]{1,0:T(8,128)(2,1)S(1)}, bf16[288,576]{1,0:T(8,128)(2,1)S(1)}, u32[]{:S(2)}, u32[]{:S(2)}) collective-permute-start(bf16[288,576]{1,0:T(8,128)(2,1)S(1)} %collective-permute-done), channel_id=1, source_target_pairs={{0,1},{1,2},{2,3},{3,4},{4,5},{5,6},{6,7},{7,0},{8,9},{9,10},{10,1... | collective-permute-start | bytes 995336 | tf_op jit(solution)/shard_map/ppermute | solution.py:99
  41.0 74.2 %copy-start.24 = (bf16[288,576]{1,0:T(8,128)(2,1)}, bf16[288,576]{1,0:T(8,128)(2,1)S(1)}, u32[]{:S(2)}) copy-start(bf16[288,576]{1,0:T(8,128)(2,1)S(1)} %collective-permute-done.8) | copy-start | bytes 995332
  41.0 19.3 %collective-permute-start.9 = (bf16[288,576]{1,0:T(8,128)(2,1)S(1)}, bf16[288,576]{1,0:T(8,128)(2,1)S(1)}, u32[]{:S(2)}, u32[]{:S(2)}) collective-permute-start(bf16[288,576]{1,0:T(8,128)(2,1)S(1)} %collective-permute-done.8), channel_id=1, source_target_pairs={{0,1},{1,2},{2,3},{3,4},{4,5},{5,6},{6,7},{7,0},{8,9},{9,10},{10,1... | collective-permute-start | bytes 995336 | tf_op jit(solution)/shard_map/ppermute | solution.py:99
  48.9 66.3 %copy-start.23 = (bf16[288,576]{1,0:T(8,128)(2,1)}, bf16[288,576]{1,0:T(8,128)(2,1)S(1)}, u32[]{:S(2)}) copy-start(bf16[288,576]{1,0:T(8,128)(2,1)S(1)} %collective-permute-done.1) | copy-start | bytes 995332
  48.9 14.9 %collective-permute-start.2 = (bf16[288,576]{1,0:T(8,128)(2,1)S(1)}, bf16[288,576]{1,0:T(8,128)(2,1)S(1)}, u32[]{:S(2)}, u32[]{:S(2)}) collective-permute-start(bf16[288,576]{1,0:T(8,128)(2,1)S(1)} %collective-permute-done.1), channel_id=1, source_target_pairs={{0,1},{1,2},{2,3},{3,4},{4,5},{5,6},{6,7},{7,0},{8,9},{9,10},{10,1... | collective-permute-start | bytes 995336 | tf_op jit(solution)/shard_map/ppermute | solution.py:99
  48.9 224.8 %reduce-scatter.10.cloned.1.call-start = ((), (), s32[]{:S(2)}) async-start(), calls=%async_computation.10 | async-start | bytes 3981312
  60.3 54.9 %copy-start.26 = (bf16[288,576]{1,0:T(8,128)(2,1)}, bf16[288,576]{1,0:T(8,128)(2,1)S(1)}, u32[]{:S(2)}) copy-start(bf16[288,576]{1,0:T(8,128)(2,1)S(1)} %collective-permute-done.9) | copy-start | bytes 995332
  60.3 14.2 %collective-permute-start.10 = (bf16[288,576]{1,0:T(8,128)(2,1)S(1)}, bf16[288,576]{1,0:T(8,128)(2,1)S(1)}, u32[]{:S(2)}, u32[]{:S(2)}) collective-permute-start(bf16[288,576]{1,0:T(8,128)(2,1)S(1)} %collective-permute-done.9), channel_id=1, source_target_pairs={{0,1},{1,2},{2,3},{3,4},{4,5},{5,6},{6,7},{7,0},{8,9},{9,10},{10,1... | collective-permute-start | bytes 995336 | tf_op jit(solution)/shard_map/ppermute | solution.py:99
  63.8 51.3 %copy-start.25 = (bf16[288,576]{1,0:T(8,128)(2,1)}, bf16[288,576]{1,0:T(8,128)(2,1)S(1)}, u32[]{:S(2)}) copy-start(bf16[288,576]{1,0:T(8,128)(2,1)S(1)} %collective-permute-done.2) | copy-start | bytes 995332
  63.9 18.5 %collective-permute-start.3 = (bf16[288,576]{1,0:T(8,128)(2,1)S(1)}, bf16[288,576]{1,0:T(8,128)(2,1)S(1)}, u32[]{:S(2)}, u32[]{:S(2)}) collective-permute-start(bf16[288,576]{1,0:T(8,128)(2,1)S(1)} %collective-permute-done.2), channel_id=1, source_target_pairs={{0,1},{1,2},{2,3},{3,4},{4,5},{5,6},{6,7},{7,0},{8,9},{9,10},{10,1... | collective-permute-start | bytes 995336 | tf_op jit(solution)/shard_map/ppermute | solution.py:99
  74.4 40.8 %copy-start.28 = (bf16[288,576]{1,0:T(8,128)(2,1)}, bf16[288,576]{1,0:T(8,128)(2,1)S(1)}, u32[]{:S(2)}) copy-start(bf16[288,576]{1,0:T(8,128)(2,1)S(1)} %collective-permute-done.10) | copy-start | bytes 995332
  74.4 15.8 %collective-permute-start.11 = (bf16[288,576]{1,0:T(8,128)(2,1)S(1)}, bf16[288,576]{1,0:T(8,128)(2,1)S(1)}, u32[]{:S(2)}, u32[]{:S(2)}) collective-permute-start(bf16[288,576]{1,0:T(8,128)(2,1)S(1)} %collective-permute-done.10), channel_id=1, source_target_pairs={{0,1},{1,2},{2,3},{3,4},{4,5},{5,6},{6,7},{7,0},{8,9},{9,10},{10,1... | collective-permute-start | bytes 995336 | tf_op jit(solution)/shard_map/ppermute | solution.py:99
  82.3 32.9 %copy-start.27 = (bf16[288,576]{1,0:T(8,128)(2,1)}, bf16[288,576]{1,0:T(8,128)(2,1)S(1)}, u32[]{:S(2)}) copy-start(bf16[288,576]{1,0:T(8,128)(2,1)S(1)} %collective-permute-done.3) | copy-start | bytes 995332
  82.3 15.8 %collective-permute-start.4 = (bf16[288,576]{1,0:T(8,128)(2,1)S(1)}, bf16[288,576]{1,0:T(8,128)(2,1)S(1)}, u32[]{:S(2)}, u32[]{:S(2)}) collective-permute-start(bf16[288,576]{1,0:T(8,128)(2,1)S(1)} %collective-permute-done.3), channel_id=1, source_target_pairs={{0,1},{1,2},{2,3},{3,4},{4,5},{5,6},{6,7},{7,0},{8,9},{9,10},{10,1... | collective-permute-start | bytes 995336 | tf_op jit(solution)/shard_map/ppermute | solution.py:99
  90.2 24.1 %copy-start.30 = (bf16[288,576]{1,0:T(8,128)(2,1)}, bf16[288,576]{1,0:T(8,128)(2,1)S(1)}, u32[]{:S(2)}) copy-start(bf16[288,576]{1,0:T(8,128)(2,1)S(1)} %collective-permute-done.11) | copy-start | bytes 995332
  90.2 15.8 %collective-permute-start.12 = (bf16[288,576]{1,0:T(8,128)(2,1)S(1)}, bf16[288,576]{1,0:T(8,128)(2,1)S(1)}, u32[]{:S(2)}, u32[]{:S(2)}) collective-permute-start(bf16[288,576]{1,0:T(8,128)(2,1)S(1)} %collective-permute-done.11), channel_id=1, source_target_pairs={{0,1},{1,2},{2,3},{3,4},{4,5},{5,6},{6,7},{7,0},{8,9},{9,10},{10,1... | collective-permute-start | bytes 995336 | tf_op jit(solution)/shard_map/ppermute | solution.py:99
  98.1 17.1 %copy-start.29 = (bf16[288,576]{1,0:T(8,128)(2,1)}, bf16[288,576]{1,0:T(8,128)(2,1)S(1)}, u32[]{:S(2)}) copy-start(bf16[288,576]{1,0:T(8,128)(2,1)S(1)} %collective-permute-done.4) | copy-start | bytes 995332
  98.1 15.9 %collective-permute-start.5 = (bf16[288,576]{1,0:T(8,128)(2,1)S(1)}, bf16[288,576]{1,0:T(8,128)(2,1)}, u32[]{:S(2)}, u32[]{:S(2)}) collective-permute-start(bf16[288,576]{1,0:T(8,128)(2,1)S(1)} %collective-permute-done.4), channel_id=1, source_target_pairs={{0,1},{1,2},{2,3},{3,4},{4,5},{5,6},{6,7},{7,0},{8,9},{9,10},{10,1... | collective-permute-start | bytes 995336 | tf_op jit(solution)/shard_map/ppermute | solution.py:99
  106.0 9.2 %copy-start.31 = (bf16[288,576]{1,0:T(8,128)(2,1)}, bf16[288,576]{1,0:T(8,128)(2,1)S(1)}, u32[]{:S(2)}) copy-start(bf16[288,576]{1,0:T(8,128)(2,1)S(1)} %collective-permute-done.12) | copy-start | bytes 995332
  106.0 15.9 %collective-permute-start.13 = (bf16[288,576]{1,0:T(8,128)(2,1)S(1)}, bf16[288,576]{1,0:T(8,128)(2,1)}, u32[]{:S(2)}, u32[]{:S(2)}) collective-permute-start(bf16[288,576]{1,0:T(8,128)(2,1)S(1)} %collective-permute-done.12), channel_id=1, source_target_pairs={{0,1},{1,2},{2,3},{3,4},{4,5},{5,6},{6,7},{7,0},{8,9},{9,10},{10,1... | collective-permute-start | bytes 995336 | tf_op jit(solution)/shard_map/ppermute | solution.py:99
  114.0 15.5 %collective-permute-start.6 = (bf16[288,576]{1,0:T(8,128)(2,1)}, bf16[288,576]{1,0:T(8,128)(2,1)}, u32[]{:S(2)}, u32[]{:S(2)}) collective-permute-start(bf16[288,576]{1,0:T(8,128)(2,1)} %collective-permute-done.5), channel_id=1, source_target_pairs={{0,1},{1,2},{2,3},{3,4},{4,5},{5,6},{6,7},{7,0},{8,9},{9,10},{10,1... | collective-permute-start | bytes 995336 | tf_op jit(solution)/shard_map/ppermute | solution.py:99
  115.2 64.4 %copy-start.12 = (f32[96,64]{1,0:T(8,128)}, f32[96,64]{1,0:T(8,128)S(1)}, u32[]{:S(2)}) copy-start(f32[96,64]{1,0:T(8,128)S(1)} %get-tuple-element.51) | copy-start | bytes 73732
  115.2 14.3 %copy-start.5 = (bf16[288,576]{1,0:T(8,128)(2,1)S(1)}, bf16[288,576]{1,0:T(8,128)(2,1)}, u32[]{:S(2)}) copy-start(bf16[288,576]{1,0:T(8,128)(2,1)} %param.18) | copy-start | bytes 995332
  125.9 9.2 %copy-start.1 = (bf16[288,4608]{1,0:T(8,128)(2,1)}, bf16[288,4608]{1,0:T(8,128)(2,1)S(1)}, u32[]{:S(2)}) copy-start(bf16[288,4608]{1,0:T(8,128)(2,1)S(1)} %concatenate.57) | copy-start | bytes 7962628
  129.5 11.7 %copy-start.47 = (f32[4608]{0:T(1024)S(1)}, f32[4608]{0:T(1024)}, u32[]{:S(2)}) copy-start(f32[4608]{0:T(1024)} %param.22) | copy-start | bytes 55300
  135.0 2.8 copy-start.3
  137.8 3.3 copy-start.2
  141.2 7.0 copy-start.48
  164.3 18.9 %copy-start.17 = (bf16[3,96,2,128]{3,2,1,0:T(2,128)(2,1)}, bf16[3,96,2,128]{3,2,1,0:T(2,128)(2,1)S(1)}, u32[]{:S(2)}) copy-start(bf16[3,96,2,128]{3,2,1,0:T(2,128)(2,1)S(1)} %convert_element_type.140) | copy-start | bytes 442372
  179.6 3.0 copy-start.38
  179.6 3.0 copy-start.39
  179.6 3.0 copy-start.43
  195.7 5.9 copy-start.16
  195.8 5.9 copy-start.15
  195.8 5.9 copy-start.40
  195.8 5.9 copy-start.44
  195.8 160.5 %reduce-scatter.12.cloned.1.call-start = ((), (), s32[]{:S(2)}) async-start(), calls=%async_computation.11 | async-start | bytes 3981312
  216.1 163.4 %copy-start.4 = (bf16[288,576]{1,0:T(8,128)(2,1)S(1)}, bf16[288,576]{1,0:T(8,128)(2,1)}, u32[]{:S(2)}) copy-start(bf16[288,576]{1,0:T(8,128)(2,1)} %param.19) | copy-start | bytes 995332
  216.1 166.1 %copy-start.52 = (s32[3]{0:T(128)S(1)}, s32[3]{0:T(128)}, u32[]{:S(2)}) copy-start(s32[3]{0:T(128)} %param.20) | copy-start | bytes 40
  216.1 282.2 %all-gather.15.cloned.1.call-start = ((), (), s32[]{:S(2)}) async-start(), calls=%async_computation.9 | async-start | bytes 3317760 | tf_op jit(solution)/shard_map/all_gather | solution.py:260
  442.9 109.1 %reduce-scatter.8.cloned.1.call-start = ((), (), s32[]{:S(2)}) async-start(), calls=%async_computation.7 | async-start | bytes 1474560 | tf_op jit(solution)/shard_map/reduce_scatter | solution.py:322
  518.3 4.8 copy-start.13
  518.3 4.8 copy-start.19
  521.6 3.6 copy-start.34
  527.5 3.0 copy-start.10
  527.5 59.0 %all-reduce.5.cloned.1.call-start = ((), (), s32[]{:S(2)}) async-start(), calls=%async_computation.8 | async-start | bytes 131072 | tf_op jit(solution)/shard_map/psum | solution.py:297
  531.4 4.4 copy-start.7
  531.4 182.5 %all-reduce.7.cloned.1.call-start = ((), (), s32[]{:S(2)}) async-start(), calls=%async_computation.12 | async-start | bytes 5898240 | tf_op jit(solution)/shard_map/psum | solution.py:339
  542.0 171.9 %copy-start.6 = (bf16[288,576]{1,0:T(8,128)(2,1)S(1)}, bf16[288,576]{1,0:T(8,128)(2,1)}, u32[]{:S(2)}) copy-start(bf16[288,576]{1,0:T(8,128)(2,1)} %param.18) | copy-start | bytes 995332
  542.0 194.5 %copy-start.49 = (f32[288]{0:T(512)S(1)}, f32[288]{0:T(512)}, u32[]{:S(2)}) copy-start(f32[288]{0:T(512)} %copy-done.48) | copy-start | bytes 3460
  542.0 194.5 %copy-start.50 = (f32[288]{0:T(512)S(1)}, f32[288]{0:T(512)}, u32[]{:S(2)}) copy-start(f32[288]{0:T(512)} %get-tuple-element.45) | copy-start | bytes 3460
  (15 other events, 23.5 us)
Sparse Core Ops, SparseCore 0:
  9.6 26.7 all-gather.8
  37.9 27.1 all-gather.6
  66.7 37.4 all-gather.10
  105.6 37.4 all-gather.12
  195.9 77.8 reduce-scatter.9
  277.2 79.0 reduce-scatter.11
  443.0 55.2 all-gather.14
  527.6 24.3 reduce-scatter.7
  554.8 31.5 all-reduce.4
  589.9 123.9 all-reduce.6
